TPU v7x, 32 devices: a whole 2x2x4 slice. The times are simulated.
32 devices in a mesh: pole: 4 (over x, core), row: 4 (over z), col: 2 (over y).
Axes of the slice: x: 2, y: 2, z: 4, core: 2. Of those that a mesh axis runs over, the one named last changes fastest.
Arguments:
- anc_inverse: bfloat16 [4, 2, 4, 192, 768], P('pole', None, None, 'col', 'row'), may hold values from -6 to 6
- panel: bfloat16 [4, 2, 768, 1024], P('pole', None, ('row', 'col')), may hold values from -0.21875 to 0.21875
- pattern: int32 [8, 2], replicated, may hold values 0 or 1
- diag_inverse: bfloat16 [4, 2, 1024, 512], P('pole', None, 'col', 'row'), may hold values from -6 to 6
- pole_weights: float32 [4, 2], P('pole'), may hold values from -4 to 4
Outputs:
- inv_panel: float32 [4, 2, 768, 1024], P('pole', None, 'row', 'col')
- inv_diag: bfloat16 [4, 2, 1024, 512], P('pole', None, 'col', 'row')
- density: float32 [1024, 512], P('col', 'row')
All inputs are finite; a program needn't handle non-finite values.
Results may differ from a plain program's by a relative error of at most 0.013.
Values may be sent and summed in bfloat16 or wider, within the bound.
A program may use at most 128 MiB of HBM per device.

v0:
```python
import jax
import jax.numpy as jnp
from jax import lax
from jax.sharding import PartitionSpec as P


def complex_left(left_re, left_im, right_re, right_im):
    upper = jnp.concatenate([left_re, left_im], axis=1)
    lower = jnp.concatenate([-left_im, left_re], axis=1)
    left_side = jnp.concatenate([upper, lower], axis=0)
    right_side = jnp.concatenate([right_re, right_im], axis=0)
    product = lax.dot_general(
        left_side, right_side, (((0,), (0,)), ((), ())), preferred_element_type=jnp.float32
    )
    return product.reshape(2, left_re.shape[1], right_re.shape[1])


def body(anc_inverse, panel, pattern, diag_inverse, pole_weights):
    n_row = lax.axis_size("row")
    n_col = lax.axis_size("col")
    fine_block = lax.axis_index("row") * n_col + lax.axis_index("col")
    pattern_row = lax.dynamic_slice_in_dim(pattern, fine_block, 1, 0)
    block_rows = panel.shape[2]
    width_all = panel.shape[3]
    groups = pattern.shape[1]
    keep_mask = pattern_row.astype(jnp.bfloat16).reshape(1, 1, 1, groups, 1)
    masked = (panel.reshape(1, 2, block_rows, groups, width_all // groups) * keep_mask).reshape(
        1, 2, block_rows, width_all
    )
    local_rows = lax.all_to_all(masked, "col", split_axis=3, concat_axis=2, tiled=True)
    row_count = anc_inverse.shape[4]
    col_count = local_rows.shape[3]
    full_cols = lax.all_gather(local_rows, "row", axis=2, tiled=True)
    stacked = full_cols[0].reshape(2, n_row, block_rows * n_col, col_count)
    segment = lax.all_gather(anc_inverse, "col", axis=3, tiled=True)
    length = segment.shape[3]
    left_side = segment[0].reshape(2, n_row * length, row_count)
    right_side = stacked.reshape(2, n_row * length, col_count)
    summed = complex_left(left_side[0], left_side[1], right_side[0], right_side[1])
    result_panel = -summed
    rounded = result_panel.astype(jnp.bfloat16)
    diag_terms = complex_left(local_rows[0, 0], local_rows[0, 1], rounded[0], rounded[1])
    row_share = lax.psum_scatter(diag_terms, "row", scatter_dimension=2, tiled=True)
    inverse_diag = diag_inverse[0].astype(jnp.float32) - row_share
    pole_weight = pole_weights[0]
    density_term = pole_weight[0] * inverse_diag[1] + pole_weight[1] * inverse_diag[0]
    density = lax.psum(density_term.astype(jnp.bfloat16), "pole").astype(jnp.float32)
    return (result_panel[None], inverse_diag.astype(jnp.bfloat16)[None], density)


def solution(mesh):
    placed = (
        P("pole", None, None, "col", "row"),
        P("pole", None, ("row", "col"), None),
        P(),
        P("pole", None, "col", "row"),
        P("pole", None),
    )
    return jax.shard_map(
        body,
        mesh=mesh,
        in_specs=placed,
        out_specs=(P("pole", None, "row", "col"), P("pole", None, "col", "row"), P("col", "row")),
        check_vma=False,
    )
```

profile of v0, /device:TPU:0, one launch (start us, length us, event | category | flops | bytes accessed | tf_op | source)
XLA Modules:
  0.0 151.4 jit_solution(4732061525736366362)
XLA Ops:
  7.2 0.0 all-gather.2.cloned.1.call-start
  7.2 0.9 fusion.26
  8.1 0.1 broadcast_bitcast_fusion
  8.2 1.0 broadcast_multiply_fusion
  9.2 0.4 copy.12
  9.6 12.2 %all_to_all.18 = bf16[1,2,96,1024]{2,1,0,3:T(2,128)(2,1)S(1)} all-to-all(bf16[1,2,96,1024]{2,1,0,3:T(2,128)(2,1)S(1)} %copy.12), channel_id=1, replica_groups=mesh['pole'=4,'row'=4,'col'=2] {'col'}, dimensions={3} | all-to-all | bytes 786432 | tf_op jit(solution)/shard_map/all_to_all | solution.py:30
  21.8 0.8 copy.15
  22.6 0.8 copy.14
  23.4 0.0 reduce-scatter.2.cloned.1.call-start
  23.5 10.5 %all_gather.6 = bf16[1,2,4,192,192]{4,3,2,1,0:T(8,128)(2,1)S(1)} all-gather(bf16[1,2,4,96,192]{4,3,2,1,0:T(8,128)(2,1)S(1)} %copy-done.1), channel_id=1, replica_groups=mesh['pole'=4,'row'=4,'col'=2] {'col'}, dimensions={3}, use_global_device_ids=true | all-gather | bytes 884736 | tf_op jit(solution)/shard_map/all_gather | solution.py:35
  34.0 0.1 fusion.30
  34.1 0.1 bitcast_negate_fusion
  34.2 26.8 %all-gather.2.cloned.1.call-done = bf16[1,2,768,512]{3,2,1,0:T(8,128)(2,1)} async-done(((bf16[1,2,192,512]{3,2,1,0:T(8,128)(2,1)}), bf16[1,2,768,512]{3,2,1,0:T(8,128)(2,1)}) %all-gather.2.cloned.1.call-update) | async-done | bytes 1572880 | tf_op jit(solution)/shard_map/all_gather | solution.py:33
  61.0 1.5 slice_bitcast_fusion.1
  62.5 1.1 fusion.4
  63.6 2.1 %fusion.14 = f32[1024,512]{1,0:T(8,128)} fusion(bf16[192,512]{1,0:T(8,128)(2,1)S(1)} %get-tuple-element.10, bf16[192,512]{1,0:T(8,128)(2,1)S(1)} %fusion.29, bf16[192,512]{1,0:T(8,128)(2,1)S(1)} %get-tuple-element.9, f32[384,512]{1,0:T(8,128)S(1)} %fusion.4), kind=kOutput, calls=%fused_computation.14 | convolution fusion | flops 405995520 | bytes 3473408 | tf_op jit(solution)/shard_map/dot_general | solution.py:12
  65.7 0.0 all-reduce.2.cloned.1.call-start
  65.8 0.6 copy-done.3
  66.3 0.6 fusion.31
  67.0 41.4 %reduce-scatter.2.cloned.1.call-done = f32[2,512,128]{2,1,0:T(8,128)} async-done(((f32[2,512,512]{2,1,0:T(8,128)}), f32[2,512,128]{2,1,0:T(8,128)}) %reduce-scatter.2.cloned.1.call-update) | async-done | bytes 524304 | tf_op jit(solution)/shard_map/reduce_scatter | solution.py:43
  108.4 1.8 %convert_bitcast_fusion = (bf16[1,2,512,128]{3,2,1,0:T(8,128)(2,1)}, f32[2,512,128]{2,1,0:T(8,128)S(1)}) fusion(f32[2,512,128]{2,1,0:T(8,128)} %reduce-scatter.2.cloned.1.call-done, bf16[1,2,512,128]{3,2,1,0:T(8,128)(2,1)S(1)} %copy-done.2), kind=kLoop, calls=%fused_computation.28 | loop fusion | flops 393216 | bytes 1572864 | tf_op jit(solution)/shard_map/broadcast_in_dim | solution.py:48
  110.2 1.9 %fusion.25 = bf16[512,128]{1,0:T(8,128)(2,1)} fusion(f32[2,512,128]{2,1,0:T(8,128)S(1)} %get-tuple-element.4, f32[]{:T(128)} %bitcast.14, f32[]{:T(128)} %bitcast.13), kind=kLoop, calls=%fused_computation.32 | loop fusion | flops 262144 | bytes 655368 | tf_op jit(solution)/shard_map/convert_element_type | solution.py:47
  112.1 31.1 %all-reduce.2.cloned.1.call-done = bf16[512,128]{1,0:T(8,128)(2,1)} async-done(((bf16[512,128]{1,0:T(8,128)(2,1)}), bf16[512,128]{1,0:T(8,128)(2,1)}) %all-reduce.2.cloned.1.call-update) | async-done | bytes 131088 | tf_op jit(solution)/shard_map/psum | solution.py:47
  143.2 1.6 %convert_element_type.32 = f32[512,128]{1,0:T(8,128)} convert(bf16[512,128]{1,0:T(8,128)(2,1)} %all-reduce.2.cloned.1.call-done) | non-fusion elementwise | flops 65536 | bytes 393216 | tf_op jit(solution)/shard_map/convert_element_type | solution.py:47
  (15 shorter events, 0.1 us)
Async XLA Ops:
  7.2 53.8 %all-gather.2.cloned.1.call-start = ((), (), s32[]{:S(2)}) async-start(), calls=%async_computation.2 | async-start | bytes 1966080 | tf_op jit(solution)/shard_map/all_gather | solution.py:33
  9.6 13.9 %copy-start.1 = (bf16[1,2,4,96,192]{4,3,2,1,0:T(8,128)(2,1)S(1)}, bf16[1,2,4,96,192]{4,3,2,1,0:T(8,128)(2,1)}, u32[]{:S(2)}) copy-start(bf16[1,2,4,96,192]{4,3,2,1,0:T(8,128)(2,1)} %param.5) | copy-start | bytes 884740
  23.4 10.7 %copy-start = (bf16[1,2,2,96,512]{4,3,2,1,0:T(8,128)(2,1)S(1)}, bf16[1,2,2,96,512]{4,3,2,1,0:T(8,128)(2,1)}, u32[]{:S(2)}) copy-start(bf16[1,2,2,96,512]{4,3,2,1,0:T(8,128)(2,1)} %copy.14) | copy-start | bytes 1179652
  23.4 84.9 %reduce-scatter.2.cloned.1.call-start = ((), (), s32[]{:S(2)}) async-start(), calls=%async_computation.3 | async-start | bytes 2621440 | tf_op jit(solution)/shard_map/reduce_scatter | solution.py:43
  63.6 2.1 %copy-start.4 = (f32[384,512]{1,0:T(8,128)}, f32[384,512]{1,0:T(8,128)S(1)}, u32[]{:S(2)}) copy-start(f32[384,512]{1,0:T(8,128)S(1)} %fusion.4) | copy-start | bytes 2359300
  65.7 0.7 copy-start.3
  65.7 42.7 %copy-start.2 = (bf16[1,2,512,128]{3,2,1,0:T(8,128)(2,1)S(1)}, bf16[1,2,512,128]{3,2,1,0:T(8,128)(2,1)}, u32[]{:S(2)}) copy-start(bf16[1,2,512,128]{3,2,1,0:T(8,128)(2,1)} %param.8) | copy-start | bytes 786436
  65.7 77.5 %all-reduce.2.cloned.1.call-start = ((), (), s32[]{:S(2)}) async-start(), calls=%async_computation.4 | async-start | bytes 262144 | tf_op jit(solution)/shard_map/psum | solution.py:47
Sparse Core Ops, SparseCore 0:
  23.5 37.4 all-gather.1
  65.8 42.5 reduce-scatter.1
  112.2 30.9 all-reduce.1
where the time goes:
time: 152 us; the launch traced here: 151 us
  waiting for transfers between devices  99.4 us (65%)
  blocking collectives  22.7 us (15%)
  between operations  13.8 us (9%)
  other arithmetic  7.29 us (5%)
  local copies, waits for them, and re-layouts  4.86 us (3%)
  matrix products  3.19 us (2%)
    reduce_scatter x1, waiting for transfers between devices, body(): lax.psum_scatter(diag_terms, 'row', scatter_dimension=2, tiled=True)  41.4 us
    psum x1, waiting for transfers between devices, body(): lax.psum(density_term.astype(jnp.bfloat16), 'pole').astype(jnp.float32)  31.1 us
    all_gather x1, waiting for transfers between devices, body(): full_cols = lax.all_gather(local_rows, 'row', axis=2, tiled=True)  26.8 us
    all_to_all x1, blocking collectives, body(): lax.all_to_all(masked, 'col', split_axis=3, concat_axis=2, tiled=True)  12.2 us
    all_gather x1, blocking collectives, body(): segment = lax.all_gather(anc_inverse, 'col', axis=3, tiled=True)  10.5 us
    dot_general x2, matrix products, complex_left(): lax.dot_general(left_side, right_side, (((0,), (0,)), ((), ())), preferre...  3.19 us
  transfers between devices with their start and end apart: 3, of which 3 were waited for; matrix products, arithmetic and copies ran while one was open for 1% of the time, Pallas kernels for 0%

commit v1 on v0

--- a/solution.py
+++ b/solution.py
@@ -30,7 +30,12 @@
     local_rows = lax.all_to_all(masked, "col", split_axis=3, concat_axis=2, tiled=True)
     row_count = anc_inverse.shape[4]
     col_count = local_rows.shape[3]
-    full_cols = lax.all_gather(local_rows, "row", axis=2, tiled=True)
+    ring = [local_rows]
+    for hop in range(3):
+        ring.append(lax.ppermute(ring[-1], "row", [(dev, (dev + 1) % 4) for dev in range(4)]))
+    full_cols = jnp.roll(
+        jnp.concatenate(ring[::-1], axis=2), (lax.axis_index("row") + 1) * ring[0].shape[2], axis=2
+    )
     stacked = full_cols[0].reshape(2, n_row, block_rows * n_col, col_count)
     segment = lax.all_gather(anc_inverse, "col", axis=3, tiled=True)
     length = segment.shape[3]

time: 152 us -> 144 us (0.947)
  waiting for transfers between devices: 99.4 us -> 91 us
  starting transfers between devices: 0.12 us -> 3.39 us
  local copies, waits for them, and re-layouts: 4.86 us -> 2.66 us
    all_gather x1 -> x0, waiting for transfers between devices: 26.8 us -> none  [body(): full_cols = lax.all_gather(local_rows, 'row', axis=2, tiled=True)]
    ppermute x0 -> x3, waiting for transfers between devices: none -> 19.1 us  [body(): lax.ppermute(ring[-1], 'row', [(dev, (dev + 1) % 4) for dev in range(4)])]
    ppermute x0 -> x3, starting transfers between devices: none -> 3.31 us  [body(): lax.ppermute(ring[-1], 'row', [(dev, (dev + 1) % 4) for dev in range(4)])]
  transfers between devices with their start and end apart: 3 -> 5, of which waited for: 3 -> 4; matrix products, arithmetic and copies ran while one was open for 1% -> 1% of each run, Pallas kernels for 0% -> 0%
where the time goes in v1:
time: 144 us
  waiting for transfers between devices  91 us (63%)
  blocking collectives  22.2 us (15%)
  between operations  14.2 us (10%)
  other arithmetic  7.39 us (5%)
  starting transfers between devices  3.39 us (2%)
  matrix products  3.18 us (2%)
  local copies, waits for them, and re-layouts  2.66 us (2%)
    reduce_scatter x1, waiting for transfers between devices, body(): lax.psum_scatter(diag_terms, 'row', scatter_dimension=2, tiled=True)  40.8 us
    psum x1, waiting for transfers between devices, body(): lax.psum(density_term.astype(jnp.bfloat16), 'pole').astype(jnp.float32)  31.1 us
    ppermute x3, waiting for transfers between devices, body(): lax.ppermute(ring[-1], 'row', [(dev, (dev + 1) % 4) for dev in range(4)])  19.1 us
    all_to_all x1, blocking collectives, body(): lax.all_to_all(masked, 'col', split_axis=3, concat_axis=2, tiled=True)  12 us
    all_gather x1, blocking collectives, body(): segment = lax.all_gather(anc_inverse, 'col', axis=3, tiled=True)  10.2 us
    ppermute x3, starting transfers between devices, body(): lax.ppermute(ring[-1], 'row', [(dev, (dev + 1) % 4) for dev in range(4)])  3.31 us
    dot_general x2, matrix products, complex_left(): lax.dot_general(left_side, right_side, (((0,), (0,)), ((), ())), preferre...  3.18 us
  transfers between devices with their start and end apart: 5, of which 4 were waited for; matrix products, arithmetic and copies ran while one was open for 1% of the time, Pallas kernels for 0%

profile of v1, /device:TPU:0, one launch (start us, length us, event | category | flops | bytes accessed | tf_op | source)
XLA Modules:
  0.0 144.1 jit_solution(5131952720708407761)
XLA Ops:
  7.2 0.0 reduce-scatter.2.cloned.1.call-start
  7.2 0.9 fusion.26
  8.1 0.1 broadcast_bitcast_fusion
  8.2 1.0 broadcast_multiply_fusion
  9.2 0.4 copy.12
  9.7 12.0 %all_to_all.18 = bf16[1,2,96,1024]{2,1,0,3:T(2,128)(2,1)S(1)} all-to-all(bf16[1,2,96,1024]{2,1,0,3:T(2,128)(2,1)S(1)} %copy.12), channel_id=1, replica_groups=mesh['pole'=4,'row'=4,'col'=2] {'col'}, dimensions={3} | all-to-all | bytes 786432 | tf_op jit(solution)/shard_map/all_to_all | solution.py:30
  21.7 0.8 copy.15
  22.6 1.7 %collective-permute-start = (bf16[1,2,192,512]{3,2,1,0:T(8,128)(2,1)S(1)}, bf16[1,2,192,512]{3,2,1,0:T(8,128)(2,1)S(1)}, u32[]{:S(2)}, u32[]{:S(2)}) collective-permute-start(bf16[1,2,192,512]{3,2,1,0:T(8,128)(2,1)S(1)} %bitcast.31), channel_id=1, source_target_pairs={{0,2},{2,4},{4,6},{6,0},{1,3},{3,5},{5,7},{7,1},{8,10},{10,12},{12... | collective-permute-start | bytes 1179656 | tf_op jit(solution)/shard_map/ppermute | solution.py:35
  24.3 10.2 %all_gather.3 = bf16[1,2,4,192,192]{4,3,2,1,0:T(8,128)(2,1)S(1)} all-gather(bf16[1,2,4,96,192]{4,3,2,1,0:T(8,128)(2,1)S(1)} %copy-done), channel_id=1, replica_groups=mesh['pole'=4,'row'=4,'col'=2] {'col'}, dimensions={3}, use_global_device_ids=true | all-gather | bytes 884736 | tf_op jit(solution)/shard_map/all_gather | solution.py:40
  34.5 1.6 %collective-permute-start.1 = (bf16[1,2,192,512]{3,2,1,0:T(8,128)(2,1)S(1)}, bf16[1,2,192,512]{3,2,1,0:T(8,128)(2,1)S(1)}, u32[]{:S(2)}, u32[]{:S(2)}) collective-permute-start(bf16[1,2,192,512]{3,2,1,0:T(8,128)(2,1)S(1)} %collective-permute-done), channel_id=1, source_target_pairs={{0,2},{2,4},{4,6},{6,0},{1,3},{3,5},{5,7},{7,1},{8,10},{10,12},{12... | collective-permute-start | bytes 1179656 | tf_op jit(solution)/shard_map/ppermute | solution.py:35
  36.1 0.1 fusion.30
  36.1 0.1 bitcast_negate_fusion
  36.2 9.1 %collective-permute-done.1 = bf16[1,2,192,512]{3,2,1,0:T(8,128)(2,1)S(1)} collective-permute-done((bf16[1,2,192,512]{3,2,1,0:T(8,128)(2,1)S(1)}, bf16[1,2,192,512]{3,2,1,0:T(8,128)(2,1)S(1)}, u32[]{:S(2)}, u32[]{:S(2)}) %collective-permute-start.1) | collective-permute-done | bytes 393248 | tf_op jit(solution)/shard_map/ppermute | solution.py:35
  45.4 9.9 %collective-permute-done.2 = bf16[1,2,192,512]{3,2,1,0:T(8,128)(2,1)S(1)} collective-permute-done((bf16[1,2,192,512]{3,2,1,0:T(8,128)(2,1)S(1)}, bf16[1,2,192,512]{3,2,1,0:T(8,128)(2,1)S(1)}, u32[]{:S(2)}, u32[]{:S(2)}) %collective-permute-start.2) | collective-permute-done | bytes 393248 | tf_op jit(solution)/shard_map/ppermute | solution.py:35
  55.6 0.4 dynamic-slice_bitcast_fusion.1
  56.0 1.1 fusion.4
  57.1 2.1 %fusion.14 = f32[1024,512]{1,0:T(8,128)} fusion(bf16[192,512]{1,0:T(8,128)(2,1)S(1)} %get-tuple-element.10, bf16[192,512]{1,0:T(8,128)(2,1)S(1)} %fusion.29, bf16[192,512]{1,0:T(8,128)(2,1)S(1)} %get-tuple-element.9, f32[384,512]{1,0:T(8,128)S(1)} %fusion.4), kind=kOutput, calls=%fused_computation.14 | convolution fusion | flops 405995520 | bytes 3473408 | tf_op jit(solution)/shard_map/dot_general | solution.py:12
  59.2 0.0 all-reduce.2.cloned.1.call-start
  59.3 0.6 fusion.31
  59.9 40.8 %reduce-scatter.2.cloned.1.call-done = f32[2,512,128]{2,1,0:T(8,128)} async-done(((f32[2,512,512]{2,1,0:T(8,128)}), f32[2,512,128]{2,1,0:T(8,128)}) %reduce-scatter.2.cloned.1.call-update) | async-done | bytes 524304 | tf_op jit(solution)/shard_map/reduce_scatter | solution.py:48
  100.7 1.8 %convert_bitcast_fusion = (bf16[1,2,512,128]{3,2,1,0:T(8,128)(2,1)}, f32[2,512,128]{2,1,0:T(8,128)S(1)}) fusion(f32[2,512,128]{2,1,0:T(8,128)} %reduce-scatter.2.cloned.1.call-done, bf16[1,2,512,128]{3,2,1,0:T(8,128)(2,1)S(1)} %copy-done.1), kind=kLoop, calls=%fused_computation.28 | loop fusion | flops 393216 | bytes 1572864 | tf_op jit(solution)/shard_map/broadcast_in_dim | solution.py:53
  102.5 2.0 %fusion.25 = bf16[512,128]{1,0:T(8,128)(2,1)} fusion(f32[2,512,128]{2,1,0:T(8,128)S(1)} %get-tuple-element.4, f32[]{:T(128)} %bitcast.14, f32[]{:T(128)} %bitcast.13), kind=kLoop, calls=%fused_computation.32 | loop fusion | flops 262144 | bytes 655368 | tf_op jit(solution)/shard_map/convert_element_type | solution.py:52
  104.5 31.1 %all-reduce.2.cloned.1.call-done = bf16[512,128]{1,0:T(8,128)(2,1)} async-done(((bf16[512,128]{1,0:T(8,128)(2,1)}), bf16[512,128]{1,0:T(8,128)(2,1)}) %all-reduce.2.cloned.1.call-update) | async-done | bytes 131088 | tf_op jit(solution)/shard_map/psum | solution.py:52
  135.6 1.6 %convert_element_type.32 = f32[512,128]{1,0:T(8,128)} convert(bf16[512,128]{1,0:T(8,128)(2,1)} %all-reduce.2.cloned.1.call-done) | non-fusion elementwise | flops 65536 | bytes 393216 | tf_op jit(solution)/shard_map/convert_element_type | solution.py:52
  (24 shorter events, 0.4 us)
Async XLA Ops:
  7.2 17.1 %copy-start = (bf16[1,2,4,96,192]{4,3,2,1,0:T(8,128)(2,1)S(1)}, bf16[1,2,4,96,192]{4,3,2,1,0:T(8,128)(2,1)}, u32[]{:S(2)}) copy-start(bf16[1,2,4,96,192]{4,3,2,1,0:T(8,128)(2,1)} %param.5) | copy-start | bytes 884740
  7.2 93.5 %reduce-scatter.2.cloned.1.call-start = ((), (), s32[]{:S(2)}) async-start(), calls=%async_computation.2 | async-start | bytes 2621440 | tf_op jit(solution)/shard_map/reduce_scatter | solution.py:48
  22.6 11.9 %collective-permute-start = (bf16[1,2,192,512]{3,2,1,0:T(8,128)(2,1)S(1)}, bf16[1,2,192,512]{3,2,1,0:T(8,128)(2,1)S(1)}, u32[]{:S(2)}, u32[]{:S(2)}) collective-permute-start(bf16[1,2,192,512]{3,2,1,0:T(8,128)(2,1)S(1)} %bitcast.31), channel_id=1, source_target_pairs={{0,2},{2,4},{4,6},{6,0},{1,3},{3,5},{5,7},{7,1},{8,10},{10,12},{12... | collective-permute-start | bytes 1179656 | tf_op jit(solution)/shard_map/ppermute | solution.py:35
  34.5 10.8 %collective-permute-start.1 = (bf16[1,2,192,512]{3,2,1,0:T(8,128)(2,1)S(1)}, bf16[1,2,192,512]{3,2,1,0:T(8,128)(2,1)S(1)}, u32[]{:S(2)}, u32[]{:S(2)}) collective-permute-start(bf16[1,2,192,512]{3,2,1,0:T(8,128)(2,1)S(1)} %collective-permute-done), channel_id=1, source_target_pairs={{0,2},{2,4},{4,6},{6,0},{1,3},{3,5},{5,7},{7,1},{8,10},{10,12},{12... | collective-permute-start | bytes 1179656 | tf_op jit(solution)/shard_map/ppermute | solution.py:35
  45.3 10.0 %collective-permute-start.2 = (bf16[1,2,192,512]{3,2,1,0:T(8,128)(2,1)S(1)}, bf16[1,2,192,512]{3,2,1,0:T(8,128)(2,1)S(1)}, u32[]{:S(2)}, u32[]{:S(2)}) collective-permute-start(bf16[1,2,192,512]{3,2,1,0:T(8,128)(2,1)S(1)} %collective-permute-done.1), channel_id=1, source_target_pairs={{0,2},{2,4},{4,6},{6,0},{1,3},{3,5},{5,7},{7,1},{8,10},{10,12},{12... | collective-permute-start | bytes 1179656 | tf_op jit(solution)/shard_map/ppermute | solution.py:35
  57.1 45.4 %copy-start.3 = (f32[384,512]{1,0:T(8,128)}, f32[384,512]{1,0:T(8,128)S(1)}, u32[]{:S(2)}) copy-start(f32[384,512]{1,0:T(8,128)S(1)} %fusion.4) | copy-start | bytes 2359300
  57.1 2.2 %copy-start.2 = (f32[1,2]{1,0:T(1,128)S(1)}, f32[1,2]{1,0:T(1,128)}, u32[]{:S(2)}) copy-start(f32[1,2]{1,0:T(1,128)} %param.9) | copy-start | bytes 28
  57.1 43.6 %copy-start.1 = (bf16[1,2,512,128]{3,2,1,0:T(8,128)(2,1)S(1)}, bf16[1,2,512,128]{3,2,1,0:T(8,128)(2,1)}, u32[]{:S(2)}) copy-start(bf16[1,2,512,128]{3,2,1,0:T(8,128)(2,1)} %param.8) | copy-start | bytes 786436
  59.2 76.4 %all-reduce.2.cloned.1.call-start = ((), (), s32[]{:S(2)}) async-start(), calls=%async_computation.3 | async-start | bytes 262144 | tf_op jit(solution)/shard_map/psum | solution.py:52
Sparse Core Ops, SparseCore 0:
  59.4 41.2 reduce-scatter.1
  104.6 30.9 all-reduce.1
